TPU v7x, 16 devices: a 4x2x1 block of a 4x4x4 slice. The times are simulated.
16 devices in a mesh: dp: 2 (over y, z), tp: 8 (over x, core).
Axes of the slice: x: 4, y: 2, z: 1, core: 2. Of those that a mesh axis runs over, the one named last changes fastest.
The devices are a block of a 4x4x4 slice.
Arguments:
- x: bfloat16 [128, 7168], P('dp'), parts along dimension 0
- k_cache: bfloat16 [128, 4096, 8, 128], P('dp', None, 'tp'), parts along dimension 0
- v_cache: bfloat16 [128, 4096, 8, 128], P('dp', None, 'tp'), parts along dimension 0
- gain_a: bfloat16 [7168], replicated
- wq: bfloat16 [7168, 7168], P(None, 'tp')
- wo: bfloat16 [7168, 7168], P('tp')
- gain_m: bfloat16 [7168], replicated
- w_gate: bfloat16 [7168, 20480], P(None, 'tp')
- w_up: bfloat16 [7168, 20480], P(None, 'tp')
- w_down: bfloat16 [20480, 7168], P('tp')
Outputs:
- output: bfloat16 [128, 7168], P('dp'), parts along dimension 0
There are 2 independent parts. A program takes and returns all parts, laid end to end along the dimension named above; an argument that names none is the same for every part.
All inputs are finite; a program needn't handle non-finite values.
Results may differ from a plain program's by a relative error of at most 0.017.
Values are sent between devices in bfloat16 or wider.
A program may use at most 1.5 GiB of HBM per device.

v0:
```python
import jax
import jax.numpy as jnp
from jax import lax
from jax.sharding import PartitionSpec as P

HEAD = 128
THETA = 10000


def normed(x, gain):
    wide = x.astype(jnp.float32)
    scale = lax.rsqrt(jnp.mean(wide * wide, -1, keepdims=True) + 1e-6)
    return (wide * scale * gain.astype(jnp.float32)).astype(jnp.bfloat16)


def turned(t, place, theta):
    half = t.shape[-1] // 2
    angle = place.astype(jnp.float32)[:, None] * theta ** (-jnp.arange(half, dtype=jnp.float32) / half)
    cos, sin = jnp.cos(angle)[:, None], jnp.sin(angle)[:, None]
    a, b = t[..., :half].astype(jnp.float32), t[..., half:].astype(jnp.float32)
    return jnp.concatenate([a * cos - b * sin, b * cos + a * sin], -1).astype(jnp.bfloat16)


def matmul(a, w):
    return jnp.dot(a, w, preferred_element_type=jnp.float32).astype(jnp.bfloat16)


def einsum(form, a, b):
    return jnp.einsum(form, a.astype(jnp.float32), b.astype(jnp.float32))


def seen_by(a, wq, k_cache, v_cache, head, theta):
    batch, cache, kv_heads = k_cache.shape[:3]
    place = jnp.full((batch,), cache - 1)
    q = turned(matmul(a, wq).reshape(batch, -1, head), place, theta).reshape(batch, kv_heads, -1, head)
    scores = einsum("bgsd,bugd->bgsu", q, k_cache) * head**-0.5
    weights = jax.nn.softmax(scores, -1).astype(jnp.bfloat16)
    return einsum("bgsu,bugd->bgsd", weights, v_cache).astype(jnp.bfloat16).reshape(batch, -1)


def hidden_of(b, w_gate, w_up):
    gate = jnp.dot(b, w_gate, preferred_element_type=jnp.float32)
    up = jnp.dot(b, w_up, preferred_element_type=jnp.float32)
    return (jax.nn.silu(gate) * up).astype(jnp.bfloat16)


def solution(mesh):
    def added(t, term):
        return (t.astype(jnp.float32) + lax.psum(term.astype(jnp.bfloat16), "tp").astype(jnp.float32)).astype(jnp.bfloat16)

    def step(x, k_cache, v_cache, gain_a, wq, wo, gain_m, w_gate, w_up, w_down):
        seen = seen_by(normed(x, gain_a), wq, k_cache, v_cache, HEAD, THETA)
        h = added(x, jnp.dot(seen, wo, preferred_element_type=jnp.float32))
        return added(h, jnp.dot(hidden_of(normed(h, gain_m), w_gate, w_up), w_down, preferred_element_type=jnp.float32))

    states, cache, columns, rows_of = P("dp", None), P("dp", None, "tp", None), P(None, "tp"), P("tp", None)
    return jax.shard_map(
        step,
        mesh=mesh,
        in_specs=(states, cache, cache, P(None), columns, rows_of, P(None), columns, columns, rows_of),
        out_specs=states,
        check_vma=False,
    )
```

profile of v0, /device:TPU:113, one launch (start us, length us, event | category | flops | bytes accessed | tf_op | source)
XLA Modules:
  0.0 239.4 jit_solution(16987218951792239552)
XLA Ops:
  6.5 0.0 all-reduce.3.cloned.1.call-start
  6.6 0.7 convert_element_type.66
  7.3 1.5 fusion.9
  8.8 7.3 %convolution_convert_fusion.2 = bf16[64,896]{1,0:T(8,128)(2,1)S(1)} fusion(bf16[7168,896]{1,0:T(8,128)(2,1)} %param.14, bf16[64,7168]{1,0:T(8,128)(2,1)} %param.10, f32[7168]{0:T(1024)S(1)} %convert_element_type.66, f32[64]{0:T(128)S(1)} %add_rsqrt_fusion.1), kind=kOutput, calls=%fused_computation.30 | convolution fusion | flops 823975936 | bytes 13906176 | tf_op jit(solution)/shard_map/dot_general | solution.py:25
  16.1 0.2 reshape.67
  16.3 0.1 fusion.30
  16.4 29.1 %fusion.48 = (f32[64,7]{1,0:T(8,128)S(1)}, f32[64,7,4096]{2,1,0:T(8,128)}) fusion(bf16[64,4096,1,128]{3,1,2,0:T(8,128)(2,1)} %param.11, bf16[64,7,64]{2,1,0:T(8,128)(2,1)S(1)} %get-tuple-element.8, bf16[64,7,64]{2,1,0:T(8,128)(2,1)S(1)} %get-tuple-element.7), kind=kOutput, calls=%fused_computation.61 | convolution fusion | flops 475500544 | bytes 74565376 | tf_op jit(solution)/shard_map/sub | solution.py:37
  45.5 25.1 %fusion.17 = bf16[64,7,128]{2,1,0:T(8,128)(2,1)S(1)} fusion(bf16[64,4096,1,128]{3,1,2,0:T(8,128)(2,1)} %param.12, f32[64,7,4096]{2,1,0:T(8,128)} %get-tuple-element.10, f32[64,7]{1,0:T(8,128)S(1)} %get-tuple-element.9), kind=kOutput, calls=%fused_computation.29 | convolution fusion | flops 473489408 | bytes 74565376 | tf_op jit(solution)/shard_map/bgsu,bugd->bgsd/dot_general | solution.py:29
  70.7 0.0 copy-start.1
  70.7 0.0 copy-start
  70.7 8.0 %convolution_convert_fusion = bf16[64,7168]{1,0:T(8,128)(2,1)} fusion(bf16[896,7168]{1,0:T(8,128)(2,1)} %param.15, bf16[8,8,7,128]{3,2,1,0:T(8,128)(2,1)S(1)} %bitcast.21), kind=kOutput, calls=%fused_computation.7 | convolution fusion | flops 822542336 | bytes 13877248 | tf_op jit(solution)/shard_map/dot_general | solution.py:53
  78.7 0.1 all-reduce.3.cloned.1.call-update
  78.8 0.2 all-reduce.5.cloned.1.call-start
  79.1 0.0 copy-done.1
  79.1 54.7 %all-reduce.3.cloned.1.call-done = bf16[64,7168]{1,0:T(8,128)(2,1)} async-done(((bf16[64,7168]{1,0:T(8,128)(2,1)}), bf16[64,7168]{1,0:T(8,128)(2,1)}) %all-reduce.3.cloned.1.call-update) | async-done | bytes 917520 | tf_op jit(solution)/shard_map/psum | solution.py:49
  133.8 0.0 copy-done
  133.8 1.6 fusion.13
  135.4 14.8 %fusion.35 = f32[64,2560]{1,0:T(8,128)S(1)} fusion(bf16[7168,2560]{1,0:T(8,128)(2,1)} %param.17, bf16[64,7168]{1,0:T(8,128)(2,1)S(1)} %get-tuple-element.6, f32[7168]{0:T(1024)S(1)} %convert_element_type.77, f32[64]{0:T(128)S(1)} %add_rsqrt_fusion), kind=kOutput, calls=%fused_computation.47 | convolution fusion | flops 2350645248 | bytes 38301952 | tf_op jit(solution)/shard_map/dot_general | solution.py:42
  150.2 26.6 %convolution_convert_fusion.1 = bf16[64,7168]{1,0:T(8,128)(2,1)} fusion(bf16[2560,7168]{1,0:T(8,128)(2,1)} %param.19, bf16[7168,2560]{1,0:T(8,128)(2,1)} %param.18, f32[64,2560]{1,0:T(8,128)S(1)} %fusion.35, bf16[64,7168]{1,0:T(8,128)(2,1)S(1)} %get-tuple-element.6, f32[7168]{0:T(1024)S(1)} %convert_element_type.77, f32[64]{0:T(128)S(1)} %add_rsqrt_fusion), kind=kOutput, calls=%fused_computation.8 | convolution fusion | flops 4700897280 | bytes 75919616 | tf_op jit(solution)/shard_map/dot_general | solution.py:54
  176.8 0.1 all-reduce.5.cloned.1.call-update
  176.9 53.3 %all-reduce.5.cloned.1.call-done = bf16[64,7168]{1,0:T(8,128)(2,1)} async-done(((bf16[64,7168]{1,0:T(8,128)(2,1)}), bf16[64,7168]{1,0:T(8,128)(2,1)}) %all-reduce.5.cloned.1.call-update) | async-done | bytes 917520 | tf_op jit(solution)/shard_map/psum | solution.py:49
  230.2 2.3 fusion.16
  (4 shorter events, 0.1 us)
Async XLA Ops:
  6.5 127.2 %all-reduce.3.cloned.1.call-start = ((), (), s32[]{:S(2)}) async-start(), calls=%async_computation | async-start | bytes 1835008 | tf_op jit(solution)/shard_map/psum | solution.py:49
  70.7 8.4 %copy-start.1 = (bf16[7168]{0:T(1024)(128)(2,1)S(1)}, bf16[7168]{0:T(1024)(128)(2,1)}, u32[]{:S(2)}) copy-start(bf16[7168]{0:T(1024)(128)(2,1)} %param.16) | copy-start | bytes 43012
  70.7 63.0 %copy-start = (bf16[64,7168]{1,0:T(8,128)(2,1)S(1)}, bf16[64,7168]{1,0:T(8,128)(2,1)}, u32[]{:S(2)}) copy-start(bf16[64,7168]{1,0:T(8,128)(2,1)} %param.10) | copy-start | bytes 2752516
  78.8 151.4 %all-reduce.5.cloned.1.call-start = ((), (), s32[]{:S(2)}) async-start(), calls=%async_computation.1 | async-start | bytes 1835008 | tf_op jit(solution)/shard_map/psum | solution.py:49
Sparse Core Ops, SparseCore 0:
  78.9 54.7 all-reduce.2
  177.0 53.1 all-reduce.4
where the time goes:
time: 242 us; the launch traced here: 239 us
  matrix products  111 us (46%)
  waiting for transfers between devices  108 us (45%)
  between operations  13.5 us (6%)
  other arithmetic  6.29 us (3%)
    psum x2, waiting for transfers between devices, added(): lax.psum(term.astype(jnp.bfloat16), 'tp').astype(jnp.float32)  108 us
    sub x1, matrix products, seen_by(): weights = jax.nn.softmax(scores, -1).astype(jnp.bfloat16)  29.1 us
    dot_general x1, matrix products, step(): jnp.dot(hidden_of(normed(h, gain_m), w_gate, w_up), w_down, preferred_ele...  26.6 us
    dot_general x1, matrix products, einsum(): return jnp.einsum(form, a.astype(jnp.float32), b.astype(jnp.float32))  25.1 us
    dot_general x1, matrix products, hidden_of(): gate = jnp.dot(b, w_gate, preferred_element_type=jnp.float32)  14.8 us
    dot_general x1, matrix products, step(): h = added(x, jnp.dot(seen, wo, preferred_element_type=jnp.float32))  8.02 us
    dot_general x1, matrix products, matmul(): jnp.dot(a, w, preferred_element_type=jnp.float32).astype(jnp.bfloat16)  7.3 us
  transfers between devices with their start and end apart: 2, of which 2 were waited for; matrix products, arithmetic and copies ran while one was open for 0% of the time, Pallas kernels for 0%

commit v1 on v0

v1 whole, which is shorter than its diff:
```python
import jax
import jax.numpy as jnp
from jax import lax
from jax.experimental import pallas as pl
from jax.experimental.pallas import tpu as pltpu
from jax.sharding import PartitionSpec as P

HEAD = 128
THETA = 10000
CORES = 2
LANES = 128
TILE = 256
PAIRS = 4
GSLOTS = 10
DSLOTS = 3
MESH = pl.DeviceIdType.MESH
F32, BF16 = jnp.float32, jnp.bfloat16


def dot(a, b):
    return jnp.dot(a, b, preferred_element_type=F32)


def layer_kernel(n, x_hbm, k_hbm, v_hbm, gains, trig, wq_hbm, wo_hbm, wg_hbm, wu_hbm, wd_hbm, out, states, act, h, slots, q, seen, score_a, score_b, hidden, own, a_send, a_recv, b_send, b_recv, x_sem, g_sem, o_sem, k_sem, v_sem, d_sem, a_ssem, a_rsem, b_ssem, b_rsem, c_ssem, c_rsem, p_ssem, p_rsem, y_sem):
    rows, d = x_hbm.shape
    batch, cache = k_hbm.shape[:2]
    width = wq_hbm.shape[1]
    heads = width // HEAD
    ff = wg_hbm.shape[1]
    chips = n // CORES
    chunk = n * LANES
    chunks = d // chunk
    half = chunk // CORES
    pairs = batch // 2
    group = slots.shape[1] // width
    wq_tiles = pl.cdiv(width, TILE)
    wo_first = wq_tiles
    wo_tiles = d // TILE
    wo_slots = pl.cdiv(wo_tiles, group)
    mlp_first = wo_first + wo_slots
    mlp_tiles = 2 * (ff // TILE)

    me = lax.axis_index("tp")
    chip, core = me // CORES, me % CORES
    partner = chip * CORES + (1 - core)

    def chip_at(step):
        return lax.rem(chip + step + chips, chips)

    def wq_copy(t):
        w = min(TILE, width - t * TILE)
        return pltpu.make_async_copy(wq_hbm.at[:, pl.ds(t * TILE, w)], slots.at[t, :, pl.ds(0, w)], g_sem.at[t])

    def wo_place(t):
        return wo_first + t // group, pl.multiple_of((t % group) * width, LANES)

    def wo_copy(t):
        slot, row = wo_place(t)
        return pltpu.make_async_copy(wo_hbm.at[:, pl.ds(pl.multiple_of(t * TILE, TILE), TILE)], slots.at[slot, pl.ds(row, width)], o_sem.at[t])

    def mlp_slot(t):
        return lax.rem(t + mlp_first, GSLOTS)

    def mlp_copy(w_hbm, t):
        slot = mlp_slot(t)
        return pltpu.make_async_copy(w_hbm.at[:, pl.ds(pl.multiple_of((t // 2) * TILE, TILE), TILE)], slots.at[slot], g_sem.at[slot])

    def mlp_start(j):
        mlp_copy(wg_hbm, 2 * j).start()
        mlp_copy(wu_hbm, 2 * j + 1).start()

    x_copy = pltpu.make_async_copy(x_hbm, states, x_sem)
    x_copy.start()
    for t in range(wq_tiles):
        wq_copy(t).start()

    def normed(src, gain_row):
        squares = jnp.zeros((rows, LANES), F32)
        for c in range(d // LANES):
            wide = src[:, c * LANES : (c + 1) * LANES].astype(F32)
            squares += wide * wide
        scale = lax.rsqrt(jnp.sum(squares, -1, keepdims=True) / d + 1e-6)
        for c in range(d // LANES):
            at = slice(c * LANES, (c + 1) * LANES)
            act[:, at] = (src[:, at].astype(F32) * scale * gains[gain_row : gain_row + 1, at]).astype(BF16)

    def attention(keys, values):
        def k_copy(p):
            slot = lax.rem(p, PAIRS)
            return pltpu.make_async_copy(k_hbm.at[pl.ds(2 * p, 2)], keys.at[slot], k_sem.at[slot])

        def v_copy(p):
            slot = lax.rem(p, PAIRS)
            return pltpu.make_async_copy(v_hbm.at[pl.ds(2 * p, 2)], values.at[slot], v_sem.at[slot])

        for p in range(PAIRS):
            k_copy(p).start()
            v_copy(p).start()

        @pl.loop(0, wo_tiles)
        def _(t):
            wo_copy(t).start()

        barrier = pltpu.get_barrier_semaphore()
        pl.semaphore_signal(barrier, inc=1, device_id={"tp": partner}, device_id_type=MESH)
        for step in range(1, chips):
            pl.semaphore_signal(barrier, inc=1, device_id={"tp": chip_at(step) * CORES + core}, device_id_type=MESH)

        x_copy.wait()
        normed(states, 0)
        for t in range(wq_tiles):
            wq_copy(t).wait()
            w = min(TILE, width - t * TILE)
            qt = dot(act[...], slots[t, :, :w]).astype(BF16).astype(F32)
            for i in range(w // HEAD):
                one = qt[:, i * HEAD : (i + 1) * HEAD]
                turned = one * trig[0:1] + pltpu.roll(one, HEAD // 2, 1) * trig[1:2]
                q[pl.ds(t * (TILE // HEAD) + i, rows, stride=8), :] = turned.astype(BF16).astype(F32)
        for i in range(heads, 8):
            q[pl.ds(i, rows, stride=8), :] = jnp.zeros((rows, HEAD), F32)

        step_keys = 512

        def scores(p, dst):
            slot = lax.rem(p, PAIRS)
            first = q[pl.ds(pl.multiple_of(16 * p, 16), 8), :]
            second = q[pl.ds(pl.multiple_of(16 * p + 8, 8), 8), :]
            zero = jnp.zeros_like(first)
            both = jnp.concatenate([jnp.concatenate([first, zero], 1), jnp.concatenate([zero, second], 1)], 0).astype(BF16)
            for c in range(0, cache, step_keys):
                at = slice(c, c + step_keys)
                k2 = jnp.concatenate([keys[slot, 0, at], keys[slot, 1, at]], 1)
                dst[:, at] = lax.dot_general(both, k2, (((1,), (1,)), ((), ())), preferred_element_type=F32)

        def weighted(p, src):
            slot = lax.rem(p, PAIRS)
            s = src[...]
            e = jnp.exp((s - jnp.max(s, -1, keepdims=True)) * HEAD**-0.5)
            weights = (e * (1 / jnp.sum(e, -1, keepdims=True))).astype(BF16)
            v2 = jnp.concatenate([values[slot, 0], values[slot, 1]], 1)
            o = dot(weights, v2)
            seen[pl.ds(pl.multiple_of(16 * p, 16), 8), :] = o[:8, :HEAD]
            seen[pl.ds(pl.multiple_of(16 * p + 8, 8), 8), :] = o[8:, HEAD:]

        k_copy(0).wait()
        scores(0, score_a)
        k_copy(PAIRS).start()

        trips = pairs // 2
        ahead = (trips - 1) - mlp_first_pairs

        def trip(i, last):
            p = 2 * i
            k_copy(p + 1).wait()
            if not last:
                k_copy(p + 2).wait()
            v_copy(p).wait()
            v_copy(p + 1).wait()
            weighted(p, score_a)
            scores(p + 1, score_b)
            if not last:
                scores(p + 2, score_a)
            weighted(p + 1, score_b)

        @pl.loop(0, trips - 1)
        def _(i):
            trip(i, False)

            @pl.when(2 * i + PAIRS + 1 < pairs)
            def _():
                for s in range(2):
                    v_copy(2 * i + PAIRS + s).start()

            @pl.when(2 * i + PAIRS + 2 < pairs)
            def _():
                k_copy(2 * i + PAIRS + 1).start()
                k_copy(2 * i + PAIRS + 2).start()

            @pl.when(2 * i + PAIRS + 2 == pairs)
            def _():
                k_copy(2 * i + PAIRS + 1).start()

            @pl.when(i >= ahead)
            def _():
                mlp_start(i - ahead)

        trip(trips - 1, True)

    free_first = (GSLOTS - wo_slots) // 2
    mlp_first_pairs = free_first

    def summed(compute, residual, result, lag_b, lag_c, lag_d):
        def columns(c, step):
            return pl.ds(pl.multiple_of(c * chunk + core * half + chip_at(step) * LANES, LANES), LANES)

        def a_copy(c):
            return pltpu.make_async_remote_copy(a_send.at[c], a_recv.at[c], a_ssem.at[c], a_rsem.at[c], device_id={"tp": partner}, device_id_type=MESH)

        def b_copy(c, step):
            to = chip_at(step)
            return pltpu.make_async_remote_copy(b_send.at[c, step - 1], b_recv.at[c, step - 1], b_ssem.at[c, step - 1], b_rsem.at[c, step - 1], device_id={"tp": to * CORES + core}, device_id_type=MESH)

        def c_copy(c, step):
            part = result.at[:, columns(c, 0)]
            return pltpu.make_async_remote_copy(part, part, c_ssem.at[c, step - 1], c_rsem.at[c, step - 1], device_id={"tp": chip_at(step) * CORES + core}, device_id_type=MESH)

        def p_copy(c, step):
            part = result.at[:, columns(c, -step)]
            return pltpu.make_async_remote_copy(part, part, p_ssem.at[c, step], p_rsem.at[c, step], device_id={"tp": partner}, device_id_type=MESH)

        def stage_a(c):
            term = compute(c)
            low, high = term[:, :half], term[:, half:]
            own[c] = jnp.where(core == 0, low, high)
            a_send[c] = jnp.where(core == 0, high, low).astype(BF16)
            a_copy(c).start()

        def stage_b(c):
            a_copy(c).wait_recv()
            own[c] = own[c] + a_recv[c].astype(F32)
            for step in range(1, chips):
                b_send[c, step - 1] = own[c, :, pl.ds(pl.multiple_of(chip_at(step) * LANES, LANES), LANES)].astype(BF16)
                b_copy(c, step).start()

        def stage_c(c):
            total = own[c, :, pl.ds(pl.multiple_of(chip * LANES, LANES), LANES)]
            for step in range(1, chips):
                b_copy(c, step).wait_recv()
                total += b_recv[c, step - 1].astype(F32)
            mine = columns(c, 0)
            result[:, mine] = (residual[:, mine].astype(F32) + total).astype(BF16)
            for step in range(1, chips):
                c_copy(c, step).start()
            p_copy(c, 0).start()

        def stage_d(c):
            for step in range(1, chips):
                c_copy(c, step).wait_recv()
                p_copy(c, step).start()

        @pl.loop(0, chunks + lag_d)
        def _(i):
            for stage, lag in ((stage_a, 0), (stage_b, lag_b), (stage_c, lag_c), (stage_d, lag_d)):
                pl.when((i >= lag) & (i < chunks + lag))(lambda stage=stage, lag=lag: stage(i - lag))

        def finish(c):
            for step in range(chips):
                p_copy(c, step).wait_recv()

        def drain(c):
            a_copy(c).wait_send()
            for step in range(1, chips):
                b_copy(c, step).wait_send()
                c_copy(c, step).wait_send()
            for step in range(chips):
                p_copy(c, step).wait_send()

        return finish, drain

    def rest(down):
        def d_copy(c):
            slot = lax.rem(c, DSLOTS)
            return pltpu.make_async_copy(wd_hbm.at[:, pl.ds(pl.multiple_of(c * chunk, chunk), chunk)], down.at[slot], d_sem.at[slot])

        for c in range(DSLOTS):
            d_copy(c).start()

        pl.semaphore_wait(pltpu.get_barrier_semaphore(), chips)

        for i in range(heads):
            hidden[:, i * HEAD : (i + 1) * HEAD] = seen[pl.ds(i, rows, stride=8), :].astype(BF16)

        def wo_term(c):
            parts = []
            for i in range(chunk // TILE):
                t = c * (chunk // TILE) + i
                wo_copy(t).wait()
                slot, row = wo_place(t)
                parts.append(dot(hidden[:, :width], slots[slot, pl.ds(row, width)]))
            term = jnp.concatenate(parts, 1)

            @pl.when(c == chunks - 1)
            def _():
                @pl.loop(free_first, GSLOTS // 2)
                def _(j):
                    mlp_start(j)

            return term

        finish, drain = summed(wo_term, states, h, 2, chunks, chunks + 4)

        @pl.loop(0, chunks)
        def _(c):
            finish(c)
            drain(c)

        normed(h, 1)

        @pl.loop(0, mlp_tiles // 2)
        def _(j):
            mlp_copy(wg_hbm, 2 * j).wait()
            mlp_copy(wu_hbm, 2 * j + 1).wait()
            gate = dot(act[...], slots[mlp_slot(2 * j)])
            up = dot(act[...], slots[mlp_slot(2 * j + 1)])
            hidden[:, pl.ds(pl.multiple_of(j * TILE, TILE), TILE)] = (gate * (1 / (1 + jnp.exp(-gate))) * up).astype(BF16)

            @pl.when(2 * j + GSLOTS < mlp_tiles)
            def _():
                mlp_start(j + GSLOTS // 2)

        def down_term(c):
            d_copy(c).wait()
            term = dot(hidden[...], down[lax.rem(c, DSLOTS)])

            @pl.when(c + DSLOTS < chunks)
            def _():
                d_copy(c + DSLOTS).start()

            return term

        finish, drain = summed(down_term, h, states, 1, 3, 5)

        def y_copy(c):
            at = pl.ds(pl.multiple_of(c * chunk, chunk), chunk)
            return pltpu.make_async_copy(states.at[:, at], out.at[:, at], y_sem.at[c])

        @pl.loop(0, chunks)
        def _(c):
            finish(c)
            y_copy(c).start()

        @pl.loop(0, chunks)
        def _(c):
            drain(c)
            y_copy(c).wait()

    pl.run_scoped(attention, pltpu.VMEM((PAIRS, 2, cache, HEAD), BF16), pltpu.VMEM((PAIRS, 2, cache, HEAD), BF16))
    pl.run_scoped(rest, pltpu.VMEM((DSLOTS, ff, chunk), BF16))


def solution(mesh):
    n = mesh.shape["tp"]

    def step(x, k_cache, v_cache, gain_a, wq, wo, gain_m, w_gate, w_up, w_down):
        rows, d = x.shape
        batch, cache, kv_heads, head = k_cache.shape
        ff = w_gate.shape[1]
        chips = n // CORES
        chunk = n * LANES
        chunks = d // chunk
        half = head // 2
        angle = jnp.full((1,), cache - 1).astype(F32)[:, None] * THETA ** (-jnp.arange(half, dtype=F32) / half)
        cos, sin = jnp.cos(angle), jnp.sin(angle)
        trig = jnp.concatenate([jnp.concatenate([cos, cos], 1), jnp.concatenate([-sin, sin], 1)], 0)
        gains = jnp.stack([gain_a, gain_m]).astype(F32)
        dma, vmem = pltpu.SemaphoreType.DMA, pltpu.VMEM
        in_hbm = pl.BlockSpec(memory_space=pl.ANY)
        in_vmem = pl.BlockSpec(memory_space=pltpu.VMEM)
        return pl.pallas_call(
            lambda *refs: layer_kernel(n, *refs),
            out_shape=jax.ShapeDtypeStruct((rows, d), x.dtype),
            in_specs=[in_hbm] * 3 + [in_vmem] * 2 + [in_hbm] * 5,
            out_specs=in_hbm,
            scratch_shapes=[
                vmem((rows, d), BF16),
                vmem((rows, d), BF16),
                vmem((rows, d), BF16),
                vmem((GSLOTS, d, TILE), BF16),
                vmem((batch * 8, head), F32),
                vmem((batch * 8, head), F32),
                vmem((16, cache), F32),
                vmem((16, cache), F32),
                vmem((rows, ff), BF16),
                vmem((chunks, rows, chunk // CORES), F32),
                vmem((chunks, rows, chunk // CORES), BF16),
                vmem((chunks, rows, chunk // CORES), BF16),
                vmem((chunks, chips - 1, rows, LANES), BF16),
                vmem((chunks, chips - 1, rows, LANES), BF16),
                dma,
                dma((GSLOTS,)),
                dma((d // TILE,)),
                dma((PAIRS,)),
                dma((PAIRS,)),
                dma((DSLOTS,)),
                dma((chunks,)),
                dma((chunks,)),
                dma((chunks, chips - 1)),
                dma((chunks, chips - 1)),
                dma((chunks, chips - 1)),
                dma((chunks, chips - 1)),
                dma((chunks, chips)),
                dma((chunks, chips)),
                dma((chunks,)),
            ],
            compiler_params=pltpu.CompilerParams(collective_id=0, has_side_effects=True, vmem_limit_bytes=67_043_328),
            name="decoder_layer",
        )(x, k_cache.reshape(batch, cache, head), v_cache.reshape(batch, cache, head), gains, trig, wq, wo, w_gate, w_up, w_down)

    states, cache, columns, rows_of = P("dp", None), P("dp", None, "tp", None), P(None, "tp"), P("tp", None)
    return jax.shard_map(
        step,
        mesh=mesh,
        in_specs=(states, cache, cache, P(None), columns, rows_of, P(None), columns, columns, rows_of),
        out_specs=states,
        check_vma=False,
    )
```

time: 242 us -> 122 us (0.50); the launches traced: 239 us -> 122 us
  Pallas kernels: 0 us -> 117 us
  matrix products: 111 us -> 0 us
  waiting for transfers between devices: 108 us -> 0 us
  between operations: 13.5 us -> 0.03 us
  other arithmetic: 6.29 us -> 1.46 us
  local copies, waits for them, and re-layouts: 0.17 us -> 3.62 us
    pallas_call x0 -> x1, Pallas kernels: none -> 117 us  [step(): pl.pallas_call(lambda *refs: layer_kernel(n, *refs), out_shape=jax.ShapeD...]
    psum x2 -> x0, waiting for transfers between devices: 108 us -> none  [added(): lax.psum(term.astype(jnp.bfloat16), 'tp').astype(jnp.float32)]
    dot_general x5 -> x0, matrix products: 81.9 us -> none  [the longest x1 26.6 us: step(): jnp.dot(hidden_of(normed(h, gain_m), w_gate, w_up), w_down, preferred_ele...]
    sub x1 -> x0, matrix products: 29.1 us -> none  [seen_by(): weights = jax.nn.softmax(scores, -1).astype(jnp.bfloat16)]
    reduce_sum x2 -> x0, other arithmetic: 3.06 us -> none  [normed(): scale = lax.rsqrt(jnp.mean(wide * wide, -1, keepdims=True) + 1e-06)]
  transfers between devices with their start and end apart: 2 -> 0, of which waited for: 2 -> 0; matrix products, arithmetic and copies ran while one was open for 0% -> 0% of each run, Pallas kernels for 0% -> 0%
where the time goes in v1:
time: 122 us
  Pallas kernels  117 us (96%)
  local copies, waits for them, and re-layouts  3.62 us (3%)
  other arithmetic  1.46 us (1%)
    pallas_call x1, Pallas kernels, step(): pl.pallas_call(lambda *refs: layer_kernel(n, *refs), out_shape=jax.ShapeD...  117 us

profile of v1, /device:TPU:113, one launch (start us, length us, event | category | flops | bytes accessed | tf_op | source)
XLA Modules:
  0.0 122.0 jit_solution(6553546916203110706)
XLA Ops:
  0.0 0.1 fusion.2
  0.1 0.1 fusion
  0.1 0.7 maximum_maximum_fusion.refs_4_
  0.8 0.7 stack.9
  1.5 0.7 stack.10
  2.2 0.7 maximum_convert_fusion.refs_3_
  2.9 116.8 %decoder_layer.1 = bf16[64,7168]{1,0:T(8,128)(2,1)} custom-call(bf16[64,7168]{1,0:T(8,128)(2,1)} %refs_0_.1, bf16[64,4096,128]{2,1,0:T(8,128)(2,1)} %bitcast.refs_1_, bf16[64,4096,128]{2,1,0:T(8,128)(2,1)} %bitcast.1.refs_2_, f32[2,7168]{1,0:T(2,128)} %maximum_convert_fusion.refs_3_, f32[2,128]{1,0:T(2,128)} %maximum_maximum_fusion.refs_4_, ...), custom_call_target="tpu_custom_call" | custom-call | tf_op jit(solution)/shard_map/decoder_layer/pallas_call | solution.py:359
  119.8 2.2 %copy.12 = bf16[64,7168]{1,0:T(8,128)(2,1)} copy(bf16[64,7168]{1,0:T(8,128)(2,1)} %decoder_layer.1) | data formatting | bytes 1835008

commit v2 on v1

v2 whole, which is shorter than its diff:
```python
import jax
import jax.numpy as jnp
from jax import lax
from jax.experimental import pallas as pl
from jax.experimental.pallas import tpu as pltpu
from jax.sharding import PartitionSpec as P

HEAD = 128
THETA = 10000
CORES = 2
LANES = 128
TILE = 256
PAIRS = 5
GSLOTS = 10
DSLOTS = 3
H_LAGS = (0, 3, 10, 17)
Y_LAGS = (0, 1, 4, 7)
MESH = pl.DeviceIdType.MESH
F32, BF16 = jnp.float32, jnp.bfloat16
scope = jax.named_scope


def dot(a, b):
    return jnp.dot(a, b, preferred_element_type=F32)


def layer_kernel(n, x_hbm, k_hbm, v_hbm, gain_a_hbm, gain_m_hbm, cos, sin, wq_hbm, wo_hbm, wg_hbm, wu_hbm, wd_hbm, out, states, act, h, gains, slots, q, seen, score_a, score_b, hidden, own, a_send, a_recv, b_send, b_recv, x_sem, gain_sem, g_sem, o_sem, k_sem, v_sem, d_sem, a_rsem, b_rsem, c_rsem, p_rsem, send_sem, y_sem):
    rows, d = x_hbm.shape
    batch, cache = k_hbm.shape[:2]
    width = wq_hbm.shape[1]
    heads = width // HEAD
    ff = wg_hbm.shape[1]
    chips = n // CORES
    chunk = n * LANES
    chunks = d // chunk
    half = chunk // CORES
    pairs = batch // 2
    trips = pairs // 2
    wq_tiles = pl.cdiv(width, TILE)
    tall = width * (chunk // TILE)
    per_slot = slots.shape[1] // tall
    wo_first = wq_tiles
    wo_slots = pl.cdiv(chunks, per_slot)
    mlp_first = wo_first + wo_slots
    mlp_tiles = 2 * (ff // TILE)
    free_first = (GSLOTS - wo_slots) // 2

    me = lax.axis_index("tp")
    chip, core = me // CORES, me % CORES
    partner = chip * CORES + (1 - core)

    def chip_at(step):
        return lax.rem(chip + step + chips, chips)

    def wq_copy(t):
        w = min(TILE, width - t * TILE)
        return pltpu.make_async_copy(wq_hbm.at[:, pl.ds(t * TILE, w)], slots.at[t, :, pl.ds(0, w)], g_sem.at[t])

    def wo_place(c):
        return wo_first + c // per_slot, (c % per_slot) * tall

    def wo_start(c):
        slot, row = wo_place(c)
        for i in range(chunk // TILE):
            at = pl.ds(pl.multiple_of(row + i * width, LANES), width)
            pltpu.make_async_copy(wo_hbm.at[:, pl.ds(pl.multiple_of(c * chunk + i * TILE, TILE), TILE)], slots.at[slot, at], o_sem.at[c]).start()

    def wo_wait(c):
        slot, row = wo_place(c)
        block = slots.at[slot, pl.ds(pl.multiple_of(row, LANES), tall)]
        pltpu.make_async_copy(block, block, o_sem.at[c]).wait()

    def mlp_slot(t):
        return lax.rem(t + mlp_first, GSLOTS)

    def mlp_copy(w_hbm, t):
        slot = mlp_slot(t)
        return pltpu.make_async_copy(w_hbm.at[:, pl.ds(pl.multiple_of((t // 2) * TILE, TILE), TILE)], slots.at[slot], g_sem.at[slot])

    def mlp_start(j):
        mlp_copy(wg_hbm, 2 * j).start()
        mlp_copy(wu_hbm, 2 * j + 1).start()

    x_copy = pltpu.make_async_copy(x_hbm, states, x_sem)
    x_copy.start()
    gain_copies = [pltpu.make_async_copy(g, gains.at[i], gain_sem.at[i]) for i, g in enumerate((gain_a_hbm, gain_m_hbm))]
    for copy in gain_copies:
        copy.start()
    for t in range(wq_tiles):
        wq_copy(t).start()

    def normed(src, which):
        squares = jnp.zeros((rows, LANES), F32)
        for c in range(d // LANES):
            wide = src[:, c * LANES : (c + 1) * LANES].astype(F32)
            squares += wide * wide
        scale = lax.rsqrt(jnp.sum(squares, -1, keepdims=True) / d + 1e-6)
        gain = gains[which].astype(F32)
        for c in range(d // LANES):
            at = slice(c * LANES, (c + 1) * LANES)
            act[:, at] = (src[:, at].astype(F32) * scale * gain[c : c + 1]).astype(BF16)

    class Summed:
        def __init__(self, name, index, first, count, compute, residual, result):
            self.name, self.index, self.rows, self.compute = name, index, pl.ds(first, count), compute
            self.residual, self.result = residual, result

        def columns(self, c, step):
            return pl.ds(pl.multiple_of(c * chunk + core * half + chip_at(step) * LANES, LANES), LANES)

        def remote(self, src, dst, stage, sem, to):
            return pltpu.make_async_remote_copy(src, dst, send_sem.at[self.index, stage], sem, device_id={"tp": to}, device_id_type=MESH)

        def arrived(self, ref, sem):
            self.remote(ref, ref, 0, sem, partner).wait_recv()

        def stage_a(self, c):
            with scope(self.name + "_term"):
                term = self.compute(c)
            low, high = term[:, :half], term[:, half:]
            own[c, self.rows] = jnp.where(core == 0, low, high)
            a_send[c, self.rows] = jnp.where(core == 0, high, low).astype(BF16)
            self.remote(a_send.at[c, self.rows], a_recv.at[c, self.rows], 0, a_rsem.at[self.index, c], partner).start()

        def stage_b(self, c):
            with scope(self.name + "_a_wait"):
                self.arrived(a_recv.at[c, self.rows], a_rsem.at[self.index, c])
            own[c, self.rows] = own[c, self.rows] + a_recv[c, self.rows].astype(F32)
            for step in range(1, chips):
                b_send[c, step - 1, self.rows] = own[c, self.rows, pl.ds(pl.multiple_of(chip_at(step) * LANES, LANES), LANES)].astype(BF16)
                self.remote(b_send.at[c, step - 1, self.rows], b_recv.at[c, step - 1, self.rows], 1, b_rsem.at[self.index, c], chip_at(step) * CORES + core).start()

        def stage_c(self, c):
            total = own[c, self.rows, pl.ds(pl.multiple_of(chip * LANES, LANES), LANES)]
            with scope(self.name + "_b_wait"):
                self.arrived(b_recv.at[c, :, self.rows], b_rsem.at[self.index, c])
            for step in range(1, chips):
                total += b_recv[c, step - 1, self.rows].astype(F32)
            mine = self.columns(c, 0)
            self.result[self.rows, mine] = (self.residual[self.rows, mine].astype(F32) + total).astype(BF16)
            part = self.result.at[self.rows, mine]
            for step in range(1, chips):
                self.remote(part, part, 2, c_rsem.at[self.index, c], chip_at(step) * CORES + core).start()
            self.remote(part, part, 3, p_rsem.at[self.index, c], partner).start()

        def stage_d(self, c):
            with scope(self.name + "_c_wait"):
                self.arrived(b_recv.at[c, :, self.rows], c_rsem.at[self.index, c])
            for step in range(1, chips):
                part = self.result.at[self.rows, self.columns(c, -step)]
                self.remote(part, part, 3, p_rsem.at[self.index, c], partner).start()

        def stages(self, i, lags):
            for stage, lag in zip((self.stage_a, self.stage_b, self.stage_c, self.stage_d), lags):
                pl.when((i >= lag) & (i < chunks + lag))(lambda stage=stage, lag=lag: stage(i - lag))

        def finish(self, c):
            with scope(self.name + "_p_wait"):
                other = pl.ds(pl.multiple_of(c * chunk + (1 - core) * half, LANES), half)
                self.arrived(self.result.at[self.rows, other], p_rsem.at[self.index, c])

        def drain(self):
            for stage, sent in enumerate((a_send.at[:, self.rows], b_send.at[:, :, self.rows], b_send.at[:, :, self.rows], a_send.at[:, self.rows])):
                self.remote(sent, sent, stage, x_sem, partner).wait_send()

    def gather_heads(first, count):
        for i in range(heads):
            hidden[first : first + count, i * HEAD : (i + 1) * HEAD] = seen[pl.ds(first * 8 + i, count, stride=8), :].astype(BF16)

    def wo_term(first, count):
        def term(c):
            slot, row = wo_place(c)
            a = hidden[first : first + count, :width]
            return jnp.concatenate([dot(a, slots[slot, pl.ds(pl.multiple_of(row + i * width, LANES), width)]) for i in range(chunk // TILE)], 1)

        return term

    early, late = rows // 2, rows - rows // 2
    sums = [Summed("h0", 0, 0, early, wo_term(0, early), states, h), Summed("h1", 1, early, late, wo_term(early, late), states, h)]
    early_trip = trips // 2 - 1
    early_lags = tuple(early_trip + lag for lag in (0, 1, 3, 5))

    def attention(keys, values):
        def k_copy(p):
            slot = lax.rem(p, PAIRS)
            return pltpu.make_async_copy(k_hbm.at[pl.ds(2 * p, 2)], keys.at[slot], k_sem.at[slot])

        def v_copy(p):
            slot = lax.rem(p, PAIRS)
            return pltpu.make_async_copy(v_hbm.at[pl.ds(2 * p, 2)], values.at[slot], v_sem.at[slot])

        for p in range(PAIRS):
            k_copy(p).start()
            v_copy(p).start()

        @pl.loop(0, chunks)
        def _(c):
            wo_start(c)

        barrier = pltpu.get_barrier_semaphore()
        pl.semaphore_signal(barrier, inc=1, device_id={"tp": partner}, device_id_type=MESH)
        for step in range(1, chips):
            pl.semaphore_signal(barrier, inc=1, device_id={"tp": chip_at(step) * CORES + core}, device_id_type=MESH)

        with scope("x_wait"):
            x_copy.wait()
            for copy in gain_copies:
                copy.wait()
        with scope("norm_a"):
            normed(states, 0)
        for t in range(wq_tiles):
            with scope("wq_wait"):
                wq_copy(t).wait()
            w = min(TILE, width - t * TILE)
            qt = dot(act[...], slots[t, :, :w]).astype(BF16).astype(F32)
            for i in range(w // HEAD):
                one = qt[:, i * HEAD : (i + 1) * HEAD]
                turned = one * jnp.concatenate([cos[...], cos[...]], 1) + pltpu.roll(one, HEAD // 2, 1) * jnp.concatenate([-sin[...], sin[...]], 1)
                q[pl.ds(t * (TILE // HEAD) + i, rows, stride=8), :] = turned.astype(BF16).astype(F32)
        for i in range(heads, 8):
            q[pl.ds(i, rows, stride=8), :] = jnp.zeros((rows, HEAD), F32)

        step_keys = 512

        def scores(p, dst):
            slot = lax.rem(p, PAIRS)
            first = q[pl.ds(pl.multiple_of(16 * p, 16), 8), :]
            second = q[pl.ds(pl.multiple_of(16 * p + 8, 8), 8), :]
            zero = jnp.zeros_like(first)
            both = jnp.concatenate([jnp.concatenate([first, zero], 1), jnp.concatenate([zero, second], 1)], 0).astype(BF16)
            for c in range(0, cache, step_keys):
                at = slice(c, c + step_keys)
                k2 = jnp.concatenate([keys[slot, 0, at], keys[slot, 1, at]], 1)
                dst[:, at] = lax.dot_general(both, k2, (((1,), (1,)), ((), ())), preferred_element_type=F32)

        def weighted(p, src):
            slot = lax.rem(p, PAIRS)
            s = src[...]
            e = jnp.exp((s - jnp.max(s, -1, keepdims=True)) * HEAD**-0.5)
            weights = (e * (1 / jnp.sum(e, -1, keepdims=True))).astype(BF16)
            v2 = jnp.concatenate([values[slot, 0], values[slot, 1]], 1)
            o = dot(weights, v2)
            seen[pl.ds(pl.multiple_of(16 * p, 16), 8), :] = o[:8, :HEAD]
            seen[pl.ds(pl.multiple_of(16 * p + 8, 8), 8), :] = o[8:, HEAD:]

        with scope("k0_wait"):
            k_copy(0).wait()
        with scope("scores0"):
            scores(0, score_a)
        k_copy(PAIRS).start()
        with scope("wo_wait"):
            for c in range(chunks):
                wo_wait(c)
        with scope("barrier"):
            pl.semaphore_wait(pltpu.get_barrier_semaphore(), chips)

        def trip(i, last):
            p = 2 * i
            with scope("trip_wait"):
                k_copy(p + 1).wait()
                if not last:
                    k_copy(p + 2).wait()
                v_copy(p).wait()
                v_copy(p + 1).wait()
            with scope("trip"):
                weighted(p, score_a)
                scores(p + 1, score_b)
                if not last:
                    scores(p + 2, score_a)
                weighted(p + 1, score_b)

        @pl.loop(0, trips - 1)
        def _(i):
            trip(i, False)
            for s in range(2):
                pl.when(2 * i + s + PAIRS < pairs)(lambda s=s: v_copy(2 * i + s + PAIRS).start())
                pl.when(2 * i + s + 1 + PAIRS < pairs)(lambda s=s: k_copy(2 * i + s + 1 + PAIRS).start())

            @pl.when(i >= trips - 1 - free_first)
            def _():
                mlp_start(i - (trips - 1 - free_first))

            pl.when(i == early_trip)(lambda: gather_heads(0, early))
            sums[0].stages(i, early_lags)

        trip(trips - 1, True)
        gather_heads(early, late)

    def rest(down):
        def d_copy(c):
            slot = lax.rem(c, DSLOTS)
            return pltpu.make_async_copy(wd_hbm.at[:, pl.ds(pl.multiple_of(c * chunk, chunk), chunk)], down.at[slot], d_sem.at[slot])

        for c in range(DSLOTS):
            d_copy(c).start()

        @pl.loop(0, chunks + H_LAGS[-1])
        def _(i):
            sums[1].stages(i, H_LAGS)

            @pl.when(i == chunks - 1)
            def _():
                @pl.loop(free_first, GSLOTS // 2)
                def _(j):
                    mlp_start(j)

            sums[0].stages(i + trips - 1, early_lags)

        for one in sums:
            pl.loop(0, chunks)(one.finish)
            one.drain()

        with scope("norm_m"):
            normed(h, 1)

        @pl.loop(0, mlp_tiles // 2, step=2)
        def _(j):
            with scope("mlp_wait"):
                for s in range(2):
                    mlp_copy(wg_hbm, 2 * (j + s)).wait()
                    mlp_copy(wu_hbm, 2 * (j + s) + 1).wait()
            with scope("mlp"):
                for s in range(2):
                    gate = dot(act[...], slots[mlp_slot(2 * (j + s))])
                    up = dot(act[...], slots[mlp_slot(2 * (j + s) + 1)])
                    hidden[:, pl.ds(pl.multiple_of((j + s) * TILE, TILE), TILE)] = (gate * (1 / (1 + jnp.exp(-gate))) * up).astype(BF16)

            for s in range(2):
                pl.when(2 * (j + s) + GSLOTS < mlp_tiles)(lambda s=s: mlp_start(j + s + GSLOTS // 2))

        def down_term(c):
            with scope("down_wait"):
                d_copy(c).wait()
            term = dot(hidden[...], down[lax.rem(c, DSLOTS)])

            @pl.when(c + DSLOTS < chunks)
            def _():
                d_copy(c + DSLOTS).start()

            return term

        y = Summed("y", 0, 0, rows, down_term, h, states)

        @pl.loop(0, chunks + Y_LAGS[-1])
        def _(i):
            y.stages(i, Y_LAGS)

        @pl.loop(0, chunks)
        def _(c):
            y.finish(c)
            at = pl.ds(pl.multiple_of(c * chunk, chunk), chunk)
            pltpu.make_async_copy(states.at[:, at], out.at[:, at], y_sem).start()

        with scope("y_out"):
            y.drain()
            pltpu.make_async_copy(states, out, y_sem).wait()

    pl.run_scoped(attention, pltpu.VMEM((PAIRS, 2, cache, HEAD), BF16), pltpu.VMEM((PAIRS, 2, cache, HEAD), BF16))
    pl.run_scoped(rest, pltpu.VMEM((DSLOTS, ff, chunk), BF16))


def solution(mesh):
    n = mesh.shape["tp"]

    def step(x, k_cache, v_cache, gain_a, wq, wo, gain_m, w_gate, w_up, w_down):
        rows, d = x.shape
        batch, cache, kv_heads, head = k_cache.shape
        ff = w_gate.shape[1]
        chips = n // CORES
        chunk = n * LANES
        chunks = d // chunk
        half = head // 2
        angle = jnp.full((1,), cache - 1).astype(F32)[:, None] * THETA ** (-jnp.arange(half, dtype=F32) / half)
        cos, sin = jnp.cos(angle), jnp.sin(angle)
        dma, vmem = pltpu.SemaphoreType.DMA, pltpu.VMEM
        in_hbm = pl.BlockSpec(memory_space=pl.ANY)
        in_vmem = pl.BlockSpec(memory_space=pltpu.VMEM)
        return pl.pallas_call(
            lambda *refs: layer_kernel(n, *refs),
            out_shape=jax.ShapeDtypeStruct((rows, d), x.dtype),
            in_specs=[in_hbm] * 5 + [in_vmem] * 2 + [in_hbm] * 5,
            out_specs=in_hbm,
            scratch_shapes=[
                vmem((rows, d), BF16),
                vmem((rows, d), BF16),
                vmem((rows, d), BF16),
                vmem((2, d // LANES, LANES), BF16),
                vmem((GSLOTS, d, TILE), BF16),
                vmem((batch * 8, head), F32),
                vmem((batch * 8, head), F32),
                vmem((16, cache), F32),
                vmem((16, cache), F32),
                vmem((rows, ff), BF16),
                vmem((chunks, rows, chunk // CORES), F32),
                vmem((chunks, rows, chunk // CORES), BF16),
                vmem((chunks, rows, chunk // CORES), BF16),
                vmem((chunks, chips - 1, rows, LANES), BF16),
                vmem((chunks, chips - 1, rows, LANES), BF16),
                dma,
                dma((2,)),
                dma((GSLOTS,)),
                dma((chunks,)),
                dma((PAIRS,)),
                dma((PAIRS,)),
                dma((DSLOTS,)),
                dma((2, chunks)),
                dma((2, chunks)),
                dma((2, chunks)),
                dma((2, chunks)),
                dma((2, 4)),
                dma,
            ],
            compiler_params=pltpu.CompilerParams(collective_id=0, has_side_effects=True, vmem_limit_bytes=67_043_328),
            name="decoder_layer",
        )(x, k_cache.reshape(batch, cache, head), v_cache.reshape(batch, cache, head), gain_a.reshape(-1, LANES), gain_m.reshape(-1, LANES), cos, sin, wq, wo, w_gate, w_up, w_down)

    states, cache, columns, rows_of = P("dp", None), P("dp", None, "tp", None), P(None, "tp"), P("tp", None)
    return jax.shard_map(
        step,
        mesh=mesh,
        in_specs=(states, cache, cache, P(None), columns, rows_of, P(None), columns, columns, rows_of),
        out_specs=states,
        check_vma=False,
    )
```

time: 122 us -> 115 us (0.943)
  Pallas kernels: 117 us -> 112 us
  local copies, waits for them, and re-layouts: 3.62 us -> 2.16 us
    pallas_call x1, Pallas kernels: 117 us -> 112 us  [step(): pl.pallas_call(lambda *refs: layer_kernel(n, *refs), out_shape=jax.ShapeD...]
    another operation x2 -> x0, local copies, waits for them, and re-layouts: 1.46 us -> none  [step(): gains = jnp.stack([gain_a, gain_m]).astype(F32)]
where the time goes in v2:
time: 115 us; the launch traced here: 114 us
  Pallas kernels  112 us (97%)
  local copies, waits for them, and re-layouts  2.16 us (2%)
    pallas_call x1, Pallas kernels, step(): pl.pallas_call(lambda *refs: layer_kernel(n, *refs), out_shape=jax.ShapeD...  112 us

profile of v2, /device:TPU:113, one launch (start us, length us, event | category | flops | bytes accessed | tf_op | source)
XLA Modules:
  0.0 114.4 jit_solution(1018881268150357650)
XLA Ops:
  0.0 0.6 fusion
  0.6 111.6 %decoder_layer.1 = bf16[64,7168]{1,0:T(8,128)(2,1)} custom-call(bf16[64,7168]{1,0:T(8,128)(2,1)} %refs_0_.1, bf16[64,4096,128]{2,1,0:T(8,128)(2,1)} %bitcast.refs_1_, bf16[64,4096,128]{2,1,0:T(8,128)(2,1)} %bitcast.1.refs_2_, bf16[56,128]{1,0:T(8,128)(2,1)} %bitcast.4, bf16[56,128]{1,0:T(8,128)(2,1)} %bitcast.5, f32[1,64]{1,0:T(1,128)} %get-tuple-element.6.refs_5_, ...), custom_call_target="tpu_custom_call" | custom-call | tf_op jit(solution)/shard_map/decoder_layer/pallas_call | solution.py:378
  112.2 2.2 %copy.12 = bf16[64,7168]{1,0:T(8,128)(2,1)} copy(bf16[64,7168]{1,0:T(8,128)(2,1)} %decoder_layer.1) | data formatting | bytes 1835008

commit v3 on v2

--- a/solution.py
+++ b/solution.py
@@ -12,7 +12,8 @@
 TILE = 256
 PAIRS = 5
 GSLOTS = 10
-DSLOTS = 3
+DSLOTS = 4
+REST_AT = (0, 0, 5, 9)
 H_LAGS = (0, 3, 10, 17)
 Y_LAGS = (0, 1, 4, 7)
 MESH = pl.DeviceIdType.MESH
@@ -24,7 +25,7 @@
     return jnp.dot(a, b, preferred_element_type=F32)
 
 
-def layer_kernel(n, x_hbm, k_hbm, v_hbm, gain_a_hbm, gain_m_hbm, cos, sin, wq_hbm, wo_hbm, wg_hbm, wu_hbm, wd_hbm, out, states, act, h, gains, slots, q, seen, score_a, score_b, hidden, own, a_send, a_recv, b_send, b_recv, x_sem, gain_sem, g_sem, o_sem, k_sem, v_sem, d_sem, a_rsem, b_rsem, c_rsem, p_rsem, send_sem, y_sem):
+def layer_kernel(n, x_hbm, k_hbm, v_hbm, gain_a_hbm, gain_m_hbm, cos_hbm, sin_hbm, wq_hbm, wo_hbm, wg_hbm, wu_hbm, wd_hbm, states, act, h, slots, q, score_a, score_b, hidden, own, a_send, a_recv, b_send, b_recv, gains, rope, x_sem, gain_sem, g_sem, o_sem, k_sem, v_sem, d_sem, a_rsem, b_rsem, c_rsem, p_rsem, send_sem):
     rows, d = x_hbm.shape
     batch, cache = k_hbm.shape[:2]
     width = wq_hbm.shape[1]
@@ -83,10 +84,17 @@
 
     x_copy = pltpu.make_async_copy(x_hbm, states, x_sem)
     x_copy.start()
-    gain_copies = [pltpu.make_async_copy(g, gains.at[i], gain_sem.at[i]) for i, g in enumerate((gain_a_hbm, gain_m_hbm))]
-    for copy in gain_copies:
+    small = [(gain_a_hbm, gains.at[0]), (gain_m_hbm, gains.at[1]), (cos_hbm, rope.at[0]), (sin_hbm, rope.at[1])]
+    small_copies = [pltpu.make_async_copy(src, dst, gain_sem.at[i]) for i, (src, dst) in enumerate(small)]
+    for copy in small_copies:
         copy.start()
-    for t in range(wq_tiles):
+    for t in range(2):
+        wq_copy(t).start()
+    with scope("x_wait"):
+        x_copy.wait()
+        for copy in small_copies:
+            copy.wait()
+    for t in range(2, wq_tiles):
         wq_copy(t).start()
 
     def normed(src, which):
@@ -150,9 +158,9 @@
                 part = self.result.at[self.rows, self.columns(c, -step)]
                 self.remote(part, part, 3, p_rsem.at[self.index, c], partner).start()
 
-        def stages(self, i, lags):
-            for stage, lag in zip((self.stage_a, self.stage_b, self.stage_c, self.stage_d), lags):
-                pl.when((i >= lag) & (i < chunks + lag))(lambda stage=stage, lag=lag: stage(i - lag))
+        def stages(self, i, lags, first=(0, 0, 0, 0), last=(chunks,) * 4):
+            for stage, lag, lo, hi in zip((self.stage_a, self.stage_b, self.stage_c, self.stage_d), lags, first, last):
+                pl.when((i >= lag + lo) & (i < lag + hi))(lambda stage=stage, lag=lag: stage(i - lag))
 
         def finish(self, c):
             with scope(self.name + "_p_wait"):
@@ -165,10 +173,12 @@
 
     def gather_heads(first, count):
         for i in range(heads):
-            hidden[first : first + count, i * HEAD : (i + 1) * HEAD] = seen[pl.ds(first * 8 + i, count, stride=8), :].astype(BF16)
+            hidden[first : first + count, i * HEAD : (i + 1) * HEAD] = q[pl.ds(first * 8 + i, count, stride=8), :].astype(BF16)
 
     def wo_term(first, count):
         def term(c):
+            if first == 0:
+                wo_wait(c)
             slot, row = wo_place(c)
             a = hidden[first : first + count, :width]
             return jnp.concatenate([dot(a, slots[slot, pl.ds(pl.multiple_of(row + i * width, LANES), width)]) for i in range(chunk // TILE)], 1)
@@ -179,6 +189,8 @@
     sums = [Summed("h0", 0, 0, early, wo_term(0, early), states, h), Summed("h1", 1, early, late, wo_term(early, late), states, h)]
     early_trip = trips // 2 - 1
     early_lags = tuple(early_trip + lag for lag in (0, 1, 3, 5))
+    early_done = tuple(min(max(trips - 1 - lag, 0), chunks) for lag in early_lags)
+    rest_lags = tuple(at - done for at, done in zip(REST_AT, early_done))
 
     def attention(keys, values):
         def k_copy(p):
@@ -202,21 +214,22 @@
         for step in range(1, chips):
             pl.semaphore_signal(barrier, inc=1, device_id={"tp": chip_at(step) * CORES + core}, device_id_type=MESH)
 
-        with scope("x_wait"):
-            x_copy.wait()
-            for copy in gain_copies:
-                copy.wait()
         with scope("norm_a"):
             normed(states, 0)
-        for t in range(wq_tiles):
+        cos = jnp.concatenate([rope[0], rope[0]], 1)
+        sin = jnp.concatenate([-rope[1], rope[1]], 1)
+        for pair in range(0, wq_tiles, 2):
+            tiles = range(pair, min(pair + 2, wq_tiles))
             with scope("wq_wait"):
-                wq_copy(t).wait()
-            w = min(TILE, width - t * TILE)
-            qt = dot(act[...], slots[t, :, :w]).astype(BF16).astype(F32)
-            for i in range(w // HEAD):
-                one = qt[:, i * HEAD : (i + 1) * HEAD]
-                turned = one * jnp.concatenate([cos[...], cos[...]], 1) + pltpu.roll(one, HEAD // 2, 1) * jnp.concatenate([-sin[...], sin[...]], 1)
-                q[pl.ds(t * (TILE // HEAD) + i, rows, stride=8), :] = turned.astype(BF16).astype(F32)
+                for t in tiles:
+                    wq_copy(t).wait()
+            with scope("wq"):
+                parts = [dot(act[...], slots[t, :, : min(TILE, width - t * TILE)]).astype(BF16).astype(F32) for t in tiles]
+                for t, part in zip(tiles, parts):
+                    for i in range(part.shape[1] // HEAD):
+                        one = part[:, i * HEAD : (i + 1) * HEAD]
+                        turned = one * cos + pltpu.roll(one, HEAD // 2, 1) * sin
+                        q[pl.ds(t * (TILE // HEAD) + i, rows, stride=8), :] = turned.astype(BF16).astype(F32)
         for i in range(heads, 8):
             q[pl.ds(i, rows, stride=8), :] = jnp.zeros((rows, HEAD), F32)
 
@@ -240,17 +253,14 @@
             weights = (e * (1 / jnp.sum(e, -1, keepdims=True))).astype(BF16)
             v2 = jnp.concatenate([values[slot, 0], values[slot, 1]], 1)
             o = dot(weights, v2)
-            seen[pl.ds(pl.multiple_of(16 * p, 16), 8), :] = o[:8, :HEAD]
-            seen[pl.ds(pl.multiple_of(16 * p + 8, 8), 8), :] = o[8:, HEAD:]
+            q[pl.ds(pl.multiple_of(16 * p, 16), 8), :] = o[:8, :HEAD]
+            q[pl.ds(pl.multiple_of(16 * p + 8, 8), 8), :] = o[8:, HEAD:]
 
         with scope("k0_wait"):
             k_copy(0).wait()
         with scope("scores0"):
             scores(0, score_a)
         k_copy(PAIRS).start()
-        with scope("wo_wait"):
-            for c in range(chunks):
-                wo_wait(c)
         with scope("barrier"):
             pl.semaphore_wait(pltpu.get_barrier_semaphore(), chips)
 
@@ -304,7 +314,7 @@
                 def _(j):
                     mlp_start(j)
 
-            sums[0].stages(i + trips - 1, early_lags)
+            sums[0].stages(i, rest_lags, first=early_done)
 
         for one in sums:
             pl.loop(0, chunks)(one.finish)
@@ -331,7 +341,8 @@
         def down_term(c):
             with scope("down_wait"):
                 d_copy(c).wait()
-            term = dot(hidden[...], down[lax.rem(c, DSLOTS)])
+            slot = lax.rem(c, DSLOTS)
+            term = jnp.concatenate([dot(hidden[...], down[slot, :, at : at + 256]) for at in range(0, chunk, 256)], 1)
 
             @pl.when(c + DSLOTS < chunks)
             def _():
@@ -348,12 +359,9 @@
         @pl.loop(0, chunks)
         def _(c):
             y.finish(c)
-            at = pl.ds(pl.multiple_of(c * chunk, chunk), chunk)
-            pltpu.make_async_copy(states.at[:, at], out.at[:, at], y_sem).start()
-
-        with scope("y_out"):
+
+        with scope("y_drain"):
             y.drain()
-            pltpu.make_async_copy(states, out, y_sem).wait()
 
     pl.run_scoped(attention, pltpu.VMEM((PAIRS, 2, cache, HEAD), BF16), pltpu.VMEM((PAIRS, 2, cache, HEAD), BF16))
     pl.run_scoped(rest, pltpu.VMEM((DSLOTS, ff, chunk), BF16))
@@ -374,19 +382,15 @@
         cos, sin = jnp.cos(angle), jnp.sin(angle)
         dma, vmem = pltpu.SemaphoreType.DMA, pltpu.VMEM
         in_hbm = pl.BlockSpec(memory_space=pl.ANY)
-        in_vmem = pl.BlockSpec(memory_space=pltpu.VMEM)
         return pl.pallas_call(
             lambda *refs: layer_kernel(n, *refs),
-            out_shape=jax.ShapeDtypeStruct((rows, d), x.dtype),
-            in_specs=[in_hbm] * 5 + [in_vmem] * 2 + [in_hbm] * 5,
-            out_specs=in_hbm,
+            out_shape=pltpu.VMEM((rows, d), x.dtype),
+            in_specs=[in_hbm] * 12,
+            out_specs=pl.BlockSpec(memory_space=pltpu.VMEM),
             scratch_shapes=[
                 vmem((rows, d), BF16),
                 vmem((rows, d), BF16),
-                vmem((rows, d), BF16),
-                vmem((2, d // LANES, LANES), BF16),
                 vmem((GSLOTS, d, TILE), BF16),
-                vmem((batch * 8, head), F32),
                 vmem((batch * 8, head), F32),
                 vmem((16, cache), F32),
                 vmem((16, cache), F32),
@@ -396,8 +400,10 @@
                 vmem((chunks, rows, chunk // CORES), BF16),
                 vmem((chunks, chips - 1, rows, LANES), BF16),
                 vmem((chunks, chips - 1, rows, LANES), BF16),
+                vmem((2, d // LANES, LANES), BF16),
+                vmem((2, 1, half), F32),
                 dma,
-                dma((2,)),
+                dma((4,)),
                 dma((GSLOTS,)),
                 dma((chunks,)),
                 dma((PAIRS,)),
@@ -408,9 +414,8 @@
                 dma((2, chunks)),
                 dma((2, chunks)),
                 dma((2, 4)),
-                dma,
             ],
-            compiler_params=pltpu.CompilerParams(collective_id=0, has_side_effects=True, vmem_limit_bytes=67_043_328),
+            compiler_params=pltpu.CompilerParams(collective_id=0, has_side_effects=True, vmem_limit_bytes=65_900_000),
             name="decoder_layer",
         )(x, k_cache.reshape(batch, cache, head), v_cache.reshape(batch, cache, head), gain_a.reshape(-1, LANES), gain_m.reshape(-1, LANES), cos, sin, wq, wo, w_gate, w_up, w_down)
 

time: 115 us -> 106 us (0.922)
  Pallas kernels: 112 us -> 105 us
  local copies, waits for them, and re-layouts: 2.16 us -> 0.93 us
    pallas_call x1, Pallas kernels: 112 us -> 105 us  [step(): pl.pallas_call(lambda *refs: layer_kernel(n, *refs), out_shape=pltpu.VMEM...]
    unnamed x1, local copies, waits for them, and re-layouts: 2.16 us -> 0.93 us
where the time goes in v3:
time: 106 us
  Pallas kernels  105 us (99%)
    pallas_call x1, Pallas kernels, step(): pl.pallas_call(lambda *refs: layer_kernel(n, *refs), out_shape=pltpu.VMEM...  105 us

profile of v3, /device:TPU:113, one launch (start us, length us, event | category | flops | bytes accessed | tf_op | source)
XLA Modules:
  0.0 106.0 jit_solution(2216173676425324525)
XLA Ops:
  0.0 0.6 fusion
  0.6 104.5 %decoder_layer.1 = bf16[64,7168]{1,0:T(8,128)(2,1)S(1)} custom-call(bf16[64,7168]{1,0:T(8,128)(2,1)} %refs_0_.1, bf16[64,4096,128]{2,1,0:T(8,128)(2,1)} %bitcast.refs_1_, bf16[64,4096,128]{2,1,0:T(8,128)(2,1)} %bitcast.1.refs_2_, bf16[56,128]{1,0:T(8,128)(2,1)} %bitcast.4, bf16[56,128]{1,0:T(8,128)(2,1)} %bitcast.5, f32[1,64]{1,0:T(1,128)} %get-tuple-element.6.refs_5_, ...), custom_call_target="tpu_custom_call" | custom-call | tf_op jit(solution)/shard_map/decoder_layer/pallas_call | solution.py:385
  105.1 0.9 copy.12

commit v4 on v3

--- a/solution.py
+++ b/solution.py
@@ -13,8 +13,9 @@
 PAIRS = 5
 GSLOTS = 10
 DSLOTS = 4
-REST_AT = (0, 0, 5, 9)
-H_LAGS = (0, 3, 10, 17)
+MLP_STEP = 1
+REST_AT = (0, 0, 2, 9)
+H_LAGS = (0, 2, 9, 16)
 Y_LAGS = (0, 1, 4, 7)
 MESH = pl.DeviceIdType.MESH
 F32, BF16 = jnp.float32, jnp.bfloat16
@@ -323,19 +324,19 @@
         with scope("norm_m"):
             normed(h, 1)
 
-        @pl.loop(0, mlp_tiles // 2, step=2)
+        @pl.loop(0, mlp_tiles // 2, step=MLP_STEP)
         def _(j):
             with scope("mlp_wait"):
-                for s in range(2):
+                for s in range(MLP_STEP):
                     mlp_copy(wg_hbm, 2 * (j + s)).wait()
                     mlp_copy(wu_hbm, 2 * (j + s) + 1).wait()
             with scope("mlp"):
-                for s in range(2):
+                for s in range(MLP_STEP):
                     gate = dot(act[...], slots[mlp_slot(2 * (j + s))])
                     up = dot(act[...], slots[mlp_slot(2 * (j + s) + 1)])
                     hidden[:, pl.ds(pl.multiple_of((j + s) * TILE, TILE), TILE)] = (gate * (1 / (1 + jnp.exp(-gate))) * up).astype(BF16)
 
-            for s in range(2):
+            for s in range(MLP_STEP):
                 pl.when(2 * (j + s) + GSLOTS < mlp_tiles)(lambda s=s: mlp_start(j + s + GSLOTS // 2))
 
         def down_term(c):

time: 106 us -> 103 us (0.972)
  Pallas kernels: 105 us -> 102 us
    pallas_call x1, Pallas kernels: 105 us -> 102 us  [step(): pl.pallas_call(lambda *refs: layer_kernel(n, *refs), out_shape=pltpu.VMEM...]
where the time goes in v4:
time: 103 us
  Pallas kernels  102 us (99%)
    pallas_call x1, Pallas kernels, step(): pl.pallas_call(lambda *refs: layer_kernel(n, *refs), out_shape=pltpu.VMEM...  102 us

profile of v4, /device:TPU:113, one launch (start us, length us, event | category | flops | bytes accessed | tf_op | source)
XLA Modules:
  0.0 103.3 jit_solution(5874753386217692259)
XLA Ops:
  0.0 0.6 fusion
  0.6 101.8 %decoder_layer.1 = bf16[64,7168]{1,0:T(8,128)(2,1)S(1)} custom-call(bf16[64,7168]{1,0:T(8,128)(2,1)} %refs_0_.1, bf16[64,4096,128]{2,1,0:T(8,128)(2,1)} %bitcast.refs_1_, bf16[64,4096,128]{2,1,0:T(8,128)(2,1)} %bitcast.1.refs_2_, bf16[56,128]{1,0:T(8,128)(2,1)} %bitcast.4, bf16[56,128]{1,0:T(8,128)(2,1)} %bitcast.5, f32[1,64]{1,0:T(1,128)} %get-tuple-element.6.refs_5_, ...), custom_call_target="tpu_custom_call" | custom-call | tf_op jit(solution)/shard_map/decoder_layer/pallas_call | solution.py:386
  102.4 0.9 copy.12

commit v5 on v4

--- a/solution.py
+++ b/solution.py
@@ -13,6 +13,7 @@
 PAIRS = 5
 GSLOTS = 10
 DSLOTS = 4
+WO_AHEAD = 4
 MLP_STEP = 1
 REST_AT = (0, 0, 2, 9)
 H_LAGS = (0, 2, 9, 16)
@@ -206,10 +207,6 @@
             k_copy(p).start()
             v_copy(p).start()
 
-        @pl.loop(0, chunks)
-        def _(c):
-            wo_start(c)
-
         barrier = pltpu.get_barrier_semaphore()
         pl.semaphore_signal(barrier, inc=1, device_id={"tp": partner}, device_id_type=MESH)
         for step in range(1, chips):
@@ -287,13 +284,13 @@
                 pl.when(2 * i + s + PAIRS < pairs)(lambda s=s: v_copy(2 * i + s + PAIRS).start())
                 pl.when(2 * i + s + 1 + PAIRS < pairs)(lambda s=s: k_copy(2 * i + s + 1 + PAIRS).start())
 
-            @pl.when(i >= trips - 1 - free_first)
-            def _():
-                mlp_start(i - (trips - 1 - free_first))
+            pl.when((i >= early_trip - WO_AHEAD) & (i < early_trip - WO_AHEAD + chunks))(lambda: wo_start(i - (early_trip - WO_AHEAD)))
+            pl.when(i >= trips - free_first)(lambda: mlp_start(i - (trips - free_first)))
 
             pl.when(i == early_trip)(lambda: gather_heads(0, early))
             sums[0].stages(i, early_lags)
 
+        mlp_start(free_first - 1)
         trip(trips - 1, True)
         gather_heads(early, late)
 

time: 103 us -> 102 us (level)
  Pallas kernels: 102 us -> 100 us
    pallas_call x1, Pallas kernels: 102 us -> 100 us  [step(): pl.pallas_call(lambda *refs: layer_kernel(n, *refs), out_shape=pltpu.VMEM...]
where the time goes in v5:
time: 102 us
  Pallas kernels  100 us (98%)
    pallas_call x1, Pallas kernels, step(): pl.pallas_call(lambda *refs: layer_kernel(n, *refs), out_shape=pltpu.VMEM...  100 us

profile of v5, /device:TPU:113, one launch (start us, length us, event | category | flops | bytes accessed | tf_op | source)
XLA Modules:
  0.0 102.0 jit_solution(16798527861790827745)
XLA Ops:
  0.0 0.6 fusion
  0.6 100.5 %decoder_layer.1 = bf16[64,7168]{1,0:T(8,128)(2,1)S(1)} custom-call(bf16[64,7168]{1,0:T(8,128)(2,1)} %refs_0_.1, bf16[64,4096,128]{2,1,0:T(8,128)(2,1)} %bitcast.refs_1_, bf16[64,4096,128]{2,1,0:T(8,128)(2,1)} %bitcast.1.refs_2_, bf16[56,128]{1,0:T(8,128)(2,1)} %bitcast.4, bf16[56,128]{1,0:T(8,128)(2,1)} %bitcast.5, f32[1,64]{1,0:T(1,128)} %get-tuple-element.6.refs_5_, ...), custom_call_target="tpu_custom_call" | custom-call | tf_op jit(solution)/shard_map/decoder_layer/pallas_call | solution.py:383
  101.0 0.9 copy.12

commit v6 on v5

--- a/solution.py
+++ b/solution.py
@@ -1,5 +1,6 @@
 import jax
 import jax.numpy as jnp
+import numpy as np
 from jax import lax
 from jax.experimental import pallas as pl
 from jax.experimental.pallas import tpu as pltpu
@@ -15,8 +16,6 @@
 DSLOTS = 4
 WO_AHEAD = 4
 MLP_STEP = 1
-REST_AT = (0, 0, 2, 9)
-H_LAGS = (0, 2, 9, 16)
 Y_LAGS = (0, 1, 4, 7)
 MESH = pl.DeviceIdType.MESH
 F32, BF16 = jnp.float32, jnp.bfloat16
@@ -124,13 +123,15 @@
         def arrived(self, ref, sem):
             self.remote(ref, ref, 0, sem, partner).wait_recv()
 
-        def stage_a(self, c):
+        def stage_a(self, *cs):
             with scope(self.name + "_term"):
-                term = self.compute(c)
-            low, high = term[:, :half], term[:, half:]
-            own[c, self.rows] = jnp.where(core == 0, low, high)
-            a_send[c, self.rows] = jnp.where(core == 0, high, low).astype(BF16)
-            self.remote(a_send.at[c, self.rows], a_recv.at[c, self.rows], 0, a_rsem.at[self.index, c], partner).start()
+                terms = [self.compute(c) for c in cs]
+            for c, term in zip(cs, terms):
+                low, high = term[:, :half], term[:, half:]
+                own[c, self.rows] = jnp.where(core == 0, low, high)
+                a_send[c, self.rows] = jnp.where(core == 0, high, low).astype(BF16)
+            for c in cs:
+                self.remote(a_send.at[c, self.rows], a_recv.at[c, self.rows], 0, a_rsem.at[self.index, c], partner).start()
 
         def stage_b(self, c):
             with scope(self.name + "_a_wait"):
@@ -160,9 +161,9 @@
                 part = self.result.at[self.rows, self.columns(c, -step)]
                 self.remote(part, part, 3, p_rsem.at[self.index, c], partner).start()
 
-        def stages(self, i, lags, first=(0, 0, 0, 0), last=(chunks,) * 4):
-            for stage, lag, lo, hi in zip((self.stage_a, self.stage_b, self.stage_c, self.stage_d), lags, first, last):
-                pl.when((i >= lag + lo) & (i < lag + hi))(lambda stage=stage, lag=lag: stage(i - lag))
+        def stages(self, i, lags):
+            for stage, lag in zip((self.stage_a, self.stage_b, self.stage_c, self.stage_d), lags):
+                pl.when((i >= lag) & (i < lag + chunks))(lambda stage=stage, lag=lag: stage(i - lag))
 
         def finish(self, c):
             with scope(self.name + "_p_wait"):
@@ -192,7 +193,6 @@
     early_trip = trips // 2 - 1
     early_lags = tuple(early_trip + lag for lag in (0, 1, 3, 5))
     early_done = tuple(min(max(trips - 1 - lag, 0), chunks) for lag in early_lags)
-    rest_lags = tuple(at - done for at, done in zip(REST_AT, early_done))
 
     def attention(keys, values):
         def k_copy(p):
@@ -302,17 +302,30 @@
         for c in range(DSLOTS):
             d_copy(c).start()
 
-        @pl.loop(0, chunks + H_LAGS[-1])
-        def _(i):
-            sums[1].stages(i, H_LAGS)
-
-            @pl.when(i == chunks - 1)
+        first, second = sums
+        even = chunks // 2 * 2
+
+        @pl.loop(0, even, step=2)
+        def _(c):
+            second.stage_a(c, c + 1)
+
+            @pl.when(c >= 2)
             def _():
-                @pl.loop(free_first, GSLOTS // 2)
-                def _(j):
-                    mlp_start(j)
-
-            sums[0].stages(i, rest_lags, first=early_done)
+                second.stage_b(c - 2)
+                second.stage_b(c - 1)
+
+        pl.loop(even, chunks)(second.stage_a)
+
+        @pl.loop(free_first, GSLOTS // 2)
+        def _(j):
+            mlp_start(j)
+
+        pl.loop(even - 2, even)(second.stage_b)
+        pl.loop(early_done[2], chunks)(first.stage_c)
+        pl.loop(even, chunks)(second.stage_b)
+        pl.loop(0, chunks)(second.stage_c)
+        pl.loop(early_done[3], chunks)(first.stage_d)
+        pl.loop(0, chunks)(second.stage_d)
 
         for one in sums:
             pl.loop(0, chunks)(one.finish)
@@ -376,8 +389,8 @@
         chunk = n * LANES
         chunks = d // chunk
         half = head // 2
-        angle = jnp.full((1,), cache - 1).astype(F32)[:, None] * THETA ** (-jnp.arange(half, dtype=F32) / half)
-        cos, sin = jnp.cos(angle), jnp.sin(angle)
+        angle = (cache - 1) * THETA ** (-np.arange(half) / half)
+        cos, sin = (jnp.asarray(f(angle)[None], F32) for f in (np.cos, np.sin))
         dma, vmem = pltpu.SemaphoreType.DMA, pltpu.VMEM
         in_hbm = pl.BlockSpec(memory_space=pl.ANY)
         return pl.pallas_call(

time: 102 us -> 102 us (level)
  no operation moved by 1% of the time
where the time goes in v6:
time: 102 us
  Pallas kernels  101 us (99%)
    pallas_call x1, Pallas kernels, step(): pl.pallas_call(lambda *refs: layer_kernel(n, *refs), out_shape=pltpu.VMEM...  101 us

profile of v6, /device:TPU:113, one launch (start us, length us, event | category | flops | bytes accessed | tf_op | source)
XLA Modules:
  0.0 101.6 jit_solution(12012328383287122957)
XLA Ops:
  0.0 100.7 %decoder_layer.1 = bf16[64,7168]{1,0:T(8,128)(2,1)S(1)} custom-call(bf16[64,7168]{1,0:T(8,128)(2,1)} %refs_0_.1, bf16[64,4096,128]{2,1,0:T(8,128)(2,1)} %bitcast.refs_1_, bf16[64,4096,128]{2,1,0:T(8,128)(2,1)} %bitcast.1.refs_2_, bf16[56,128]{1,0:T(8,128)(2,1)} %bitcast.4, bf16[56,128]{1,0:T(8,128)(2,1)} %bitcast.5, f32[1,64]{1,0:T(1,128)} %constant.4.clone.refs_5_, ...), custom_call_target="tpu_custom_call" | custom-call | tf_op jit(solution)/shard_map/decoder_layer/pallas_call | solution.py:396
  100.7 0.9 copy.14
